TPU v7x, 32 devices: a whole 2x2x4 slice. The times are simulated.
32 devices in a mesh: parts: 2 (over y), row: 4 (over z), col: 4 (over x, core).
Axes of the slice: x: 2, y: 2, z: 4, core: 2. Of those that a mesh axis runs over, the one named last changes fastest.
Arguments:
- state: float32 [10, 128, 512], P(None, ('parts', 'row'), 'col'), parts along dimension 1, may hold values from -5 to 5
- history: float32 [10, 128, 512], P(None, ('parts', 'row'), 'col'), parts along dimension 1, may hold values from -5 to 5
- rates: float32 [10, 10, 128, 512], P(None, None, ('parts', 'row'), 'col'), parts along dimension 2, may hold values from -2 to 2
- quadratic: float32 [10, 128, 512], P(None, ('parts', 'row'), 'col'), parts along dimension 1, may hold values from 0.1 to 1
- velocity: float32 [10, 2], replicated, may hold values from -1.5 to 1.5
- precond: float32 [10, 10, 128, 512], P(None, None, ('parts', 'row'), 'col'), parts along dimension 2, may hold values from -1 to 2, as said below
Outputs:
- updated: float32 [10, 128, 512], P(None, ('parts', 'row'), 'col'), parts along dimension 1
- lin_residual: float32 [2], P('parts'), parts along dimension 0
There are 2 independent parts, one for each index of `parts`. A program takes and returns all parts, laid end to end along the dimension named above; an argument that names none is the same for every part. Nothing has to cross between parts.
Inputs may be any that keep to these rules, and one draw needn't show every extreme that they name: `precond`: each cell's block has diagonal entries 1 plus a spread term and independent off-diagonal entries.
All inputs are finite; a program needn't handle non-finite values.
Results may differ from a plain program's by a relative error of at most 0.00011.
Values sent between devices are 32-bit elements; how exact they have to be, the bound alone decides.
No kernel may reach another device: no remote copies, remote signals or barrier semaphores. Data moves between devices by JAX's collectives and lax.ppermute only.
A program may use at most 64 MiB of HBM per device.

v0:
```python
import jax
import jax.numpy as jnp
from jax import lax
from jax.sharding import PartitionSpec as P

KRYLOV = 4
step_gamma = 0.4
tiny_eps = 1e-12


def extended(block, sides, width):
    for axis, dim in sides:
        count = lax.axis_size(axis)
        forward = [(i, i + 1) for i in range(count - 1)]
        backward = [(target, source) for source, target in forward]
        low = lax.ppermute(
            lax.slice_in_dim(block, block.shape[dim] - width, None, axis=dim), axis, forward
        )
        high = lax.ppermute(lax.slice_in_dim(block, 0, width, axis=dim), axis, backward)
        block = jnp.concatenate([low, block, high], axis=dim)
    return block


def advect(field, velocity):
    padded = extended(field, (("row", 1), ("col", 2)), 1)
    along_x = padded[:, 2:, 1:-1] - padded[:, :-2, 1:-1]
    along_y = padded[:, 1:-1, 2:] - padded[:, 1:-1, :-2]
    return -0.5 * (
        velocity[:, 0][:, None, None] * along_x + velocity[:, 1][:, None, None] * along_y
    )


def blockmul(matrix, field):
    return jnp.sum(matrix * field[None], axis=1)


def least_squares(hessen, beta):
    width = hessen.shape[1]
    rotated = jnp.zeros((width + 1,), jnp.float32).at[0].set(beta)
    upper = hessen
    for index in range(width):
        first = upper[index, index]
        second = upper[index + 1, index]
        radius = jnp.sqrt(first * first + second * second)
        cosine = first / radius
        sine = second / radius
        row_top = cosine * upper[index] + sine * upper[index + 1]
        row_low = -sine * upper[index] + cosine * upper[index + 1]
        upper = upper.at[index].set(row_top).at[index + 1].set(row_low)
        g_top = cosine * rotated[index] + sine * rotated[index + 1]
        g_low = -sine * rotated[index] + cosine * rotated[index + 1]
        rotated = rotated.at[index].set(g_top).at[index + 1].set(g_low)
    coef = jnp.zeros((width,), jnp.float32)
    for index in reversed(range(width)):
        partial_sum = jnp.sum(upper[index, index + 1 : width] * coef[index + 1 : width])
        coef = coef.at[index].set((rotated[index] - partial_sum) / upper[index, index])
    return (coef, jnp.abs(rotated[width]))


def body(state, history, rates, quadratic, velocity, precond):
    forcing = advect(state, velocity) + blockmul(rates, state) - quadratic * state * state
    rhs = -(state - history - step_gamma * forcing)
    beta = jnp.sqrt(lax.psum(jnp.sum(rhs * rhs), ("row", "col")) + tiny_eps)
    basis = [rhs / beta]
    kept = []
    hessen = jnp.zeros((KRYLOV + 1, KRYLOV), jnp.float32)
    for index in range(KRYLOV):
        direct = blockmul(precond, basis[index])
        kept.append(direct)
        jac = advect(direct, velocity) + blockmul(rates, direct) - 2.0 * quadratic * state * direct
        vector = direct - step_gamma * jac
        stacked = jnp.stack(basis)
        local_dots = jnp.sum(stacked * vector[None], axis=(1, 2, 3))
        dots, before = lax.psum((local_dots, jnp.sum(vector * vector)), ("row", "col"))
        vector = vector - jnp.sum(dots[:, None, None, None] * stacked, axis=0)
        squared = before - jnp.sum(dots * dots)
        size_new = jnp.sqrt(squared + tiny_eps)
        hessen = hessen.at[: index + 1, index].set(dots).at[index + 1, index].set(size_new)
        basis.append(vector / size_new)
    coef, lin_norm = least_squares(hessen, beta)
    combined = jnp.sum(coef[:, None, None, None] * jnp.stack(basis[:KRYLOV]), axis=0)
    correction = blockmul(precond, combined)
    return (state + correction, jnp.reshape(lin_norm, (1,)))


def solution(mesh):
    placed = (
        P(None, ("parts", "row"), "col"),
        P(None, ("parts", "row"), "col"),
        P(None, None, ("parts", "row"), "col"),
        P(None, ("parts", "row"), "col"),
        P(),
        P(None, None, ("parts", "row"), "col"),
    )
    return jax.shard_map(
        body,
        mesh=mesh,
        in_specs=placed,
        out_specs=(P(None, ("parts", "row"), "col"), P("parts")),
        check_vma=False,
    )
```

profile of v0, /device:TPU:0, one launch (start us, length us, event | category | flops | bytes accessed | tf_op | source)
XLA Modules:
  0.0 279.6 jit_solution(16215169505555502827)
XLA Ops:
  0.6 0.8 fusion.64
  1.4 1.3 collective-permute-start
  2.7 5.6 %collective-permute-start.1 = (f32[10,1,128]{2,1,0:T(1,128)S(1)}, f32[10,1,128]{2,1,0:T(1,128)S(1)}, u32[]{:S(2)}, u32[]{:S(2)}) collective-permute-start(f32[10,1,128]{2,1,0:T(1,128)S(1)} %get-tuple-element.388), channel_id=1, source_target_pairs={{0,4},{4,8},{8,12},{1,5},{5,9},{9,13},{2,6},{6,10},{10,14},{3,7},{... | collective-permute-start | bytes 15368 | tf_op jit(solution)/shard_map/ppermute | solution.py:16
  8.4 1.3 multiply_reduce_fusion.9
  10.3 0.7 and_reduce_fusion.1
  11.0 0.7 and_reduce_fusion
  12.5 1.3 collective-permute-start.2
  13.8 3.0 %collective-permute-start.3 = (f32[10,18,1]{2,1,0:T(8,128)S(1)}, f32[10,18,1]{2,1,0:T(8,128)S(1)}, u32[]{:S(2)}, u32[]{:S(2)}) collective-permute-start(f32[10,18,1]{2,1,0:T(8,128)S(1)} %get-tuple-element.379), channel_id=1, source_target_pairs={{0,1},{1,2},{2,3},{4,5},{5,6},{6,7},{8,9},{9,10},{10,11},{12,13},{... | collective-permute-start | bytes 2168 | tf_op jit(solution)/shard_map/ppermute | solution.py:16
  16.9 0.9 collective-permute-done.3
  17.8 0.8 multiply_reduce_fusion.21
  18.6 33.0 %psum.63 = f32[]{:T(128)} all-reduce(f32[]{:T(128)} %get-tuple-element.368), channel_id=1, replica_groups=mesh['parts'=2,'row'=4,'col'=4] {'row','col'}, use_global_device_ids=true, to_apply=%region_2.0 | all-reduce | flops 1 | bytes 8 | tf_op jit(solution)/shard_map/psum | solution.py:63
  52.4 1.4 collective-permute-start.4
  53.9 4.5 %collective-permute-start.5 = (f32[10,1,128]{2,1,0:T(1,128)S(1)}, f32[10,1,128]{2,1,0:T(1,128)S(1)}, u32[]{:S(2)}, u32[]{:S(2)}) collective-permute-start(f32[10,1,128]{2,1,0:T(1,128)S(1)} %get-tuple-element.386), channel_id=1, source_target_pairs={{0,4},{4,8},{8,12},{1,5},{5,9},{9,13},{2,6},{6,10},{10,14},{3,7},{... | collective-permute-start | bytes 15368 | tf_op jit(solution)/shard_map/ppermute | solution.py:16
  59.9 1.3 collective-permute-start.6
  61.2 3.0 %collective-permute-start.7 = (f32[10,18,1]{2,1,0:T(8,128)S(1)}, f32[10,18,1]{2,1,0:T(8,128)S(1)}, u32[]{:S(2)}, u32[]{:S(2)}) collective-permute-start(f32[10,18,1]{2,1,0:T(8,128)S(1)} %get-tuple-element.377), channel_id=1, source_target_pairs={{0,1},{1,2},{2,3},{4,5},{5,6},{6,7},{8,9},{9,10},{10,11},{12,13},{... | collective-permute-start | bytes 2168 | tf_op jit(solution)/shard_map/ppermute | solution.py:16
  64.3 0.9 collective-permute-done.7
  65.2 0.8 multiply_reduce_fusion.20
  66.0 31.1 %all-reduce.6 = (f32[]{:T(128)}, f32[1]{0:T(128)}) all-reduce(f32[]{:T(128)} %get-tuple-element.351, f32[1]{0:T(128)} %bitcast.2), channel_id=1, replica_groups=mesh['parts'=2,'row'=4,'col'=4] {'row','col'}, use_global_device_ids=true, to_apply=%region_8.0 | all-reduce | flops 2 | bytes 16 | tf_op jit(solution)/shard_map/psum | solution.py:74
  99.1 0.7 subtract_divide_fusion.2
  99.8 1.3 collective-permute-start.8
  101.1 4.5 %collective-permute-start.9 = (f32[10,1,128]{2,1,0:T(1,128)S(1)}, f32[10,1,128]{2,1,0:T(1,128)S(1)}, u32[]{:S(2)}, u32[]{:S(2)}) collective-permute-start(f32[10,1,128]{2,1,0:T(1,128)S(1)} %get-tuple-element.384), channel_id=1, source_target_pairs={{0,4},{4,8},{8,12},{1,5},{5,9},{9,13},{2,6},{6,10},{10,14},{3,7},{... | collective-permute-start | bytes 15368 | tf_op jit(solution)/shard_map/ppermute | solution.py:16
  105.7 1.3 collective-permute-done.9
  107.1 1.3 collective-permute-start.10
  108.4 3.0 %collective-permute-start.11 = (f32[10,18,1]{2,1,0:T(8,128)S(1)}, f32[10,18,1]{2,1,0:T(8,128)S(1)}, u32[]{:S(2)}, u32[]{:S(2)}) collective-permute-start(f32[10,18,1]{2,1,0:T(8,128)S(1)} %get-tuple-element.375), channel_id=1, source_target_pairs={{0,1},{1,2},{2,3},{4,5},{5,6},{6,7},{8,9},{9,10},{10,11},{12,13},{... | collective-permute-start | bytes 2168 | tf_op jit(solution)/shard_map/ppermute | solution.py:16
  112.4 0.8 multiply_reduce_fusion.18
  113.3 31.0 %all-reduce.5 = (f32[2]{0:T(128)S(1)}, f32[]{:T(128)}) all-reduce(f32[2]{0:T(128)S(1)} %multiply_reduce_fusion.15, f32[]{:T(128)} %get-tuple-element.364), channel_id=1, replica_groups=mesh['parts'=2,'row'=4,'col'=4] {'row','col'}, use_global_device_ids=true, to_apply=%region_13.0 | all-reduce | flops 3 | bytes 24 | tf_op jit(solution)/shard_map/psum | solution.py:74
  144.4 0.7 multiply_reduce_fusion.26
  146.6 1.3 collective-permute-start.12
  147.9 4.5 %collective-permute-start.13 = (f32[10,1,128]{2,1,0:T(1,128)S(1)}, f32[10,1,128]{2,1,0:T(1,128)S(1)}, u32[]{:S(2)}, u32[]{:S(2)}) collective-permute-start(f32[10,1,128]{2,1,0:T(1,128)S(1)} %get-tuple-element.382), channel_id=1, source_target_pairs={{0,4},{4,8},{8,12},{1,5},{5,9},{9,13},{2,6},{6,10},{10,14},{3,7},{... | collective-permute-start | bytes 15368 | tf_op jit(solution)/shard_map/ppermute | solution.py:16
  152.4 1.9 broadcast_select_fusion.2
  154.4 1.3 collective-permute-start.14
  155.8 3.0 %collective-permute-start.15 = (f32[10,18,1]{2,1,0:T(8,128)S(1)}, f32[10,18,1]{2,1,0:T(8,128)S(1)}, u32[]{:S(2)}, u32[]{:S(2)}) collective-permute-start(f32[10,18,1]{2,1,0:T(8,128)S(1)} %get-tuple-element.373), channel_id=1, source_target_pairs={{0,1},{1,2},{2,3},{4,5},{5,6},{6,7},{8,9},{9,10},{10,11},{12,13},{... | collective-permute-start | bytes 2168 | tf_op jit(solution)/shard_map/ppermute | solution.py:16
  158.9 1.4 scatter.60
  160.4 0.8 multiply_reduce_fusion.17
  161.3 30.3 %all-reduce.4 = (f32[3]{0:T(128)S(1)}, f32[]{:T(128)}) all-reduce(f32[3]{0:T(128)S(1)} %multiply_reduce_fusion.13, f32[]{:T(128)} %get-tuple-element.362), channel_id=1, replica_groups=mesh['parts'=2,'row'=4,'col'=4] {'row','col'}, use_global_device_ids=true, to_apply=%region_22.0 | all-reduce | flops 4 | bytes 32 | tf_op jit(solution)/shard_map/psum | solution.py:74
  193.7 1.3 collective-permute-start.16
  195.0 4.5 %collective-permute-start.17 = (f32[10,1,128]{2,1,0:T(1,128)S(1)}, f32[10,1,128]{2,1,0:T(1,128)S(1)}, u32[]{:S(2)}, u32[]{:S(2)}) collective-permute-start(f32[10,1,128]{2,1,0:T(1,128)S(1)} %get-tuple-element.380), channel_id=1, source_target_pairs={{0,4},{4,8},{8,12},{1,5},{5,9},{9,13},{2,6},{6,10},{10,14},{3,7},{... | collective-permute-start | bytes 15368 | tf_op jit(solution)/shard_map/ppermute | solution.py:16
  199.6 1.9 broadcast_select_fusion.1
  201.6 1.3 collective-permute-start.18
  202.9 3.0 %collective-permute-start.19 = (f32[10,18,1]{2,1,0:T(8,128)S(1)}, f32[10,18,1]{2,1,0:T(8,128)S(1)}, u32[]{:S(2)}, u32[]{:S(2)}) collective-permute-start(f32[10,18,1]{2,1,0:T(8,128)S(1)} %get-tuple-element.371), channel_id=1, source_target_pairs={{0,1},{1,2},{2,3},{4,5},{5,6},{6,7},{8,9},{9,10},{10,11},{12,13},{... | collective-permute-start | bytes 2168 | tf_op jit(solution)/shard_map/ppermute | solution.py:16
  206.0 1.4 scatter.64
  207.6 0.8 multiply_reduce_fusion.16
  208.5 30.7 %all-reduce.3 = (f32[4]{0:T(128)S(1)}, f32[]{:T(128)}) all-reduce(f32[4]{0:T(128)S(1)} %multiply_reduce_fusion.11, f32[]{:T(128)} %get-tuple-element.360), channel_id=1, replica_groups=mesh['parts'=2,'row'=4,'col'=4] {'row','col'}, use_global_device_ids=true, to_apply=%region_31.0 | all-reduce | flops 5 | bytes 40 | tf_op jit(solution)/shard_map/psum | solution.py:74
  241.1 2.0 broadcast_select_fusion
  243.1 1.3 scatter.66
  249.4 0.7 fusion.66
  272.9 0.7 multiply_reduce_fusion.23
  275.0 0.7 multiply_reduce_fusion.22
  (107 shorter events, 13.9 us)
Async XLA Ops:
  1.4 10.9 %collective-permute-start = (f32[10,1,128]{2,1,0:T(1,128)S(1)}, f32[10,1,128]{2,1,0:T(1,128)S(1)}, u32[]{:S(2)}, u32[]{:S(2)}) collective-permute-start(f32[10,1,128]{2,1,0:T(1,128)S(1)} %get-tuple-element.389), channel_id=1, source_target_pairs={{4,0},{8,4},{12,8},{5,1},{9,5},{13,9},{6,2},{10,6},{14,10},{7,3},{... | collective-permute-start | bytes 15368 | tf_op jit(solution)/shard_map/ppermute | solution.py:19
  2.7 5.6 %copy-start.5 = (f32[10,2]{0,1:T(2,128)S(1)}, f32[10,2]{0,1:T(2,128)}, u32[]{:S(2)}) copy-start(f32[10,2]{0,1:T(2,128)} %param.68) | copy-start | bytes 244
  2.7 9.6 %collective-permute-start.1 = (f32[10,1,128]{2,1,0:T(1,128)S(1)}, f32[10,1,128]{2,1,0:T(1,128)S(1)}, u32[]{:S(2)}, u32[]{:S(2)}) collective-permute-start(f32[10,1,128]{2,1,0:T(1,128)S(1)} %get-tuple-element.388), channel_id=1, source_target_pairs={{0,4},{4,8},{8,12},{1,5},{5,9},{9,13},{2,6},{6,10},{10,14},{3,7},{... | collective-permute-start | bytes 15368 | tf_op jit(solution)/shard_map/ppermute | solution.py:16
  8.4 2.0 copy-start.6
  8.4 2.7 copy-start.7
  8.4 4.0 %copy-start.2 = (f32[10,16,128]{2,1,0:T(8,128)S(1)}, f32[10,16,128]{2,1,0:T(8,128)}, u32[]{:S(2)}) copy-start(f32[10,16,128]{2,1,0:T(8,128)} %param.64) | copy-start | bytes 245764
  8.4 9.4 %copy-start.3 = (f32[10,16,128]{2,1,0:T(8,128)S(1)}, f32[10,16,128]{2,1,0:T(8,128)}, u32[]{:S(2)}) copy-start(f32[10,16,128]{2,1,0:T(8,128)} %param.67) | copy-start | bytes 245764
  8.4 9.4 %copy-start.4 = (f32[10,16,128]{2,1,0:T(8,128)S(1)}, f32[10,16,128]{2,1,0:T(8,128)}, u32[]{:S(2)}) copy-start(f32[10,16,128]{2,1,0:T(8,128)} %param.65) | copy-start | bytes 245764
  9.7 42.6 %copy-start.1 = (f32[10,10,16,128]{3,2,1,0:T(8,128)S(1)}, f32[10,10,16,128]{3,2,1,0:T(8,128)}, u32[]{:S(2)}) copy-start(f32[10,10,16,128]{3,2,1,0:T(8,128)} %param.69) | copy-start | bytes 2457604
  12.5 4.4 %collective-permute-start.2 = (f32[10,18,1]{2,1,0:T(8,128)S(1)}, f32[10,18,1]{2,1,0:T(8,128)S(1)}, u32[]{:S(2)}, u32[]{:S(2)}) collective-permute-start(f32[10,18,1]{2,1,0:T(8,128)S(1)} %get-tuple-element.378), channel_id=1, source_target_pairs={{1,0},{2,1},{3,2},{5,4},{6,5},{7,6},{9,8},{10,9},{11,10},{13,12},{... | collective-permute-start | bytes 2168 | tf_op jit(solution)/shard_map/ppermute | solution.py:19
  13.8 4.0 %collective-permute-start.3 = (f32[10,18,1]{2,1,0:T(8,128)S(1)}, f32[10,18,1]{2,1,0:T(8,128)S(1)}, u32[]{:S(2)}, u32[]{:S(2)}) collective-permute-start(f32[10,18,1]{2,1,0:T(8,128)S(1)} %get-tuple-element.379), channel_id=1, source_target_pairs={{0,1},{1,2},{2,3},{4,5},{5,6},{6,7},{8,9},{9,10},{10,11},{12,13},{... | collective-permute-start | bytes 2168 | tf_op jit(solution)/shard_map/ppermute | solution.py:16
  52.3 11.9 %copy-start = (f32[10,10,16,128]{3,2,1,0:T(8,128)S(1)}, f32[10,10,16,128]{3,2,1,0:T(8,128)}, u32[]{:S(2)}) copy-start(f32[10,10,16,128]{3,2,1,0:T(8,128)} %param.66) | copy-start | bytes 2457604
  52.4 7.2 %collective-permute-start.4 = (f32[10,1,128]{2,1,0:T(1,128)S(1)}, f32[10,1,128]{2,1,0:T(1,128)S(1)}, u32[]{:S(2)}, u32[]{:S(2)}) collective-permute-start(f32[10,1,128]{2,1,0:T(1,128)S(1)} %get-tuple-element.387), channel_id=1, source_target_pairs={{4,0},{8,4},{12,8},{5,1},{9,5},{13,9},{6,2},{10,6},{14,10},{7,3},{... | collective-permute-start | bytes 15368 | tf_op jit(solution)/shard_map/ppermute | solution.py:19
  53.9 5.9 %collective-permute-start.5 = (f32[10,1,128]{2,1,0:T(1,128)S(1)}, f32[10,1,128]{2,1,0:T(1,128)S(1)}, u32[]{:S(2)}, u32[]{:S(2)}) collective-permute-start(f32[10,1,128]{2,1,0:T(1,128)S(1)} %get-tuple-element.386), channel_id=1, source_target_pairs={{0,4},{4,8},{8,12},{1,5},{5,9},{9,13},{2,6},{6,10},{10,14},{3,7},{... | collective-permute-start | bytes 15368 | tf_op jit(solution)/shard_map/ppermute | solution.py:16
  59.9 4.4 %collective-permute-start.6 = (f32[10,18,1]{2,1,0:T(8,128)S(1)}, f32[10,18,1]{2,1,0:T(8,128)S(1)}, u32[]{:S(2)}, u32[]{:S(2)}) collective-permute-start(f32[10,18,1]{2,1,0:T(8,128)S(1)} %get-tuple-element.376), channel_id=1, source_target_pairs={{1,0},{2,1},{3,2},{5,4},{6,5},{7,6},{9,8},{10,9},{11,10},{13,12},{... | collective-permute-start | bytes 2168 | tf_op jit(solution)/shard_map/ppermute | solution.py:19
  61.2 4.0 %collective-permute-start.7 = (f32[10,18,1]{2,1,0:T(8,128)S(1)}, f32[10,18,1]{2,1,0:T(8,128)S(1)}, u32[]{:S(2)}, u32[]{:S(2)}) collective-permute-start(f32[10,18,1]{2,1,0:T(8,128)S(1)} %get-tuple-element.377), channel_id=1, source_target_pairs={{0,1},{1,2},{2,3},{4,5},{5,6},{6,7},{8,9},{9,10},{10,11},{12,13},{... | collective-permute-start | bytes 2168 | tf_op jit(solution)/shard_map/ppermute | solution.py:16
  99.8 5.9 %collective-permute-start.8 = (f32[10,1,128]{2,1,0:T(1,128)S(1)}, f32[10,1,128]{2,1,0:T(1,128)S(1)}, u32[]{:S(2)}, u32[]{:S(2)}) collective-permute-start(f32[10,1,128]{2,1,0:T(1,128)S(1)} %get-tuple-element.385), channel_id=1, source_target_pairs={{4,0},{8,4},{12,8},{5,1},{9,5},{13,9},{6,2},{10,6},{14,10},{7,3},{... | collective-permute-start | bytes 15368 | tf_op jit(solution)/shard_map/ppermute | solution.py:19
  101.1 5.9 %collective-permute-start.9 = (f32[10,1,128]{2,1,0:T(1,128)S(1)}, f32[10,1,128]{2,1,0:T(1,128)S(1)}, u32[]{:S(2)}, u32[]{:S(2)}) collective-permute-start(f32[10,1,128]{2,1,0:T(1,128)S(1)} %get-tuple-element.384), channel_id=1, source_target_pairs={{0,4},{4,8},{8,12},{1,5},{5,9},{9,13},{2,6},{6,10},{10,14},{3,7},{... | collective-permute-start | bytes 15368 | tf_op jit(solution)/shard_map/ppermute | solution.py:16
  107.1 5.2 %collective-permute-start.10 = (f32[10,18,1]{2,1,0:T(8,128)S(1)}, f32[10,18,1]{2,1,0:T(8,128)S(1)}, u32[]{:S(2)}, u32[]{:S(2)}) collective-permute-start(f32[10,18,1]{2,1,0:T(8,128)S(1)} %get-tuple-element.374), channel_id=1, source_target_pairs={{1,0},{2,1},{3,2},{5,4},{6,5},{7,6},{9,8},{10,9},{11,10},{13,12},{... | collective-permute-start | bytes 2168 | tf_op jit(solution)/shard_map/ppermute | solution.py:19
  108.4 4.0 %collective-permute-start.11 = (f32[10,18,1]{2,1,0:T(8,128)S(1)}, f32[10,18,1]{2,1,0:T(8,128)S(1)}, u32[]{:S(2)}, u32[]{:S(2)}) collective-permute-start(f32[10,18,1]{2,1,0:T(8,128)S(1)} %get-tuple-element.375), channel_id=1, source_target_pairs={{0,1},{1,2},{2,3},{4,5},{5,6},{6,7},{8,9},{9,10},{10,11},{12,13},{... | collective-permute-start | bytes 2168 | tf_op jit(solution)/shard_map/ppermute | solution.py:16
  146.6 7.7 %collective-permute-start.12 = (f32[10,1,128]{2,1,0:T(1,128)S(1)}, f32[10,1,128]{2,1,0:T(1,128)S(1)}, u32[]{:S(2)}, u32[]{:S(2)}) collective-permute-start(f32[10,1,128]{2,1,0:T(1,128)S(1)} %get-tuple-element.383), channel_id=1, source_target_pairs={{4,0},{8,4},{12,8},{5,1},{9,5},{13,9},{6,2},{10,6},{14,10},{7,3},{... | collective-permute-start | bytes 15368 | tf_op jit(solution)/shard_map/ppermute | solution.py:19
  147.9 6.4 %collective-permute-start.13 = (f32[10,1,128]{2,1,0:T(1,128)S(1)}, f32[10,1,128]{2,1,0:T(1,128)S(1)}, u32[]{:S(2)}, u32[]{:S(2)}) collective-permute-start(f32[10,1,128]{2,1,0:T(1,128)S(1)} %get-tuple-element.382), channel_id=1, source_target_pairs={{0,4},{4,8},{8,12},{1,5},{5,9},{9,13},{2,6},{6,10},{10,14},{3,7},{... | collective-permute-start | bytes 15368 | tf_op jit(solution)/shard_map/ppermute | solution.py:16
  154.4 6.0 %collective-permute-start.14 = (f32[10,18,1]{2,1,0:T(8,128)S(1)}, f32[10,18,1]{2,1,0:T(8,128)S(1)}, u32[]{:S(2)}, u32[]{:S(2)}) collective-permute-start(f32[10,18,1]{2,1,0:T(8,128)S(1)} %get-tuple-element.372), channel_id=1, source_target_pairs={{1,0},{2,1},{3,2},{5,4},{6,5},{7,6},{9,8},{10,9},{11,10},{13,12},{... | collective-permute-start | bytes 2168 | tf_op jit(solution)/shard_map/ppermute | solution.py:19
  155.8 4.7 %collective-permute-start.15 = (f32[10,18,1]{2,1,0:T(8,128)S(1)}, f32[10,18,1]{2,1,0:T(8,128)S(1)}, u32[]{:S(2)}, u32[]{:S(2)}) collective-permute-start(f32[10,18,1]{2,1,0:T(8,128)S(1)} %get-tuple-element.373), channel_id=1, source_target_pairs={{0,1},{1,2},{2,3},{4,5},{5,6},{6,7},{8,9},{9,10},{10,11},{12,13},{... | collective-permute-start | bytes 2168 | tf_op jit(solution)/shard_map/ppermute | solution.py:16
  193.7 7.8 %collective-permute-start.16 = (f32[10,1,128]{2,1,0:T(1,128)S(1)}, f32[10,1,128]{2,1,0:T(1,128)S(1)}, u32[]{:S(2)}, u32[]{:S(2)}) collective-permute-start(f32[10,1,128]{2,1,0:T(1,128)S(1)} %get-tuple-element.381), channel_id=1, source_target_pairs={{4,0},{8,4},{12,8},{5,1},{9,5},{13,9},{6,2},{10,6},{14,10},{7,3},{... | collective-permute-start | bytes 15368 | tf_op jit(solution)/shard_map/ppermute | solution.py:19
  195.0 6.5 %collective-permute-start.17 = (f32[10,1,128]{2,1,0:T(1,128)S(1)}, f32[10,1,128]{2,1,0:T(1,128)S(1)}, u32[]{:S(2)}, u32[]{:S(2)}) collective-permute-start(f32[10,1,128]{2,1,0:T(1,128)S(1)} %get-tuple-element.380), channel_id=1, source_target_pairs={{0,4},{4,8},{8,12},{1,5},{5,9},{9,13},{2,6},{6,10},{10,14},{3,7},{... | collective-permute-start | bytes 15368 | tf_op jit(solution)/shard_map/ppermute | solution.py:16
  201.6 5.9 %collective-permute-start.18 = (f32[10,18,1]{2,1,0:T(8,128)S(1)}, f32[10,18,1]{2,1,0:T(8,128)S(1)}, u32[]{:S(2)}, u32[]{:S(2)}) collective-permute-start(f32[10,18,1]{2,1,0:T(8,128)S(1)} %get-tuple-element.370), channel_id=1, source_target_pairs={{1,0},{2,1},{3,2},{5,4},{6,5},{7,6},{9,8},{10,9},{11,10},{13,12},{... | collective-permute-start | bytes 2168 | tf_op jit(solution)/shard_map/ppermute | solution.py:19
  202.9 4.6 %collective-permute-start.19 = (f32[10,18,1]{2,1,0:T(8,128)S(1)}, f32[10,18,1]{2,1,0:T(8,128)S(1)}, u32[]{:S(2)}, u32[]{:S(2)}) collective-permute-start(f32[10,18,1]{2,1,0:T(8,128)S(1)} %get-tuple-element.371), channel_id=1, source_target_pairs={{0,1},{1,2},{2,3},{4,5},{5,6},{6,7},{8,9},{9,10},{10,11},{12,13},{... | collective-permute-start | bytes 2168 | tf_op jit(solution)/shard_map/ppermute | solution.py:16
where the time goes:
time: 281 us; the launch traced here: 280 us
  blocking collectives  156 us (56%)
  starting transfers between devices  52 us (19%)
  between operations  33.8 us (12%)
  other arithmetic  19.4 us (7%)
  local copies, waits for them, and re-layouts  15 us (5%)
  waiting for transfers between devices  3.3 us (1%)
    psum x4, blocking collectives, body(): lax.psum((local_dots, jnp.sum(vector * vector)), ('row', 'col'))  123 us
    ppermute x10, starting transfers between devices, extended(): lax.ppermute(lax.slice_in_dim(block, block.shape[dim] - width, None, axis...  39 us
    psum x1, blocking collectives, body(): beta = jnp.sqrt(lax.psum(jnp.sum(rhs * rhs), ('row', 'col')) + tiny_eps)  33 us
    ppermute x10, starting transfers between devices, extended(): lax.ppermute(lax.slice_in_dim(block, 0, width, axis=dim), axis, backward)  13 us
    another operation x8, other arithmetic  7.82 us
  transfers between devices with their start and end apart: 20, of which 5 were waited for; matrix products, arithmetic and copies ran while one was open for 5% of the time, Pallas kernels for 0%

commit v1 on v0

--- a/solution.py
+++ b/solution.py
@@ -71,7 +71,7 @@
         vector = direct - step_gamma * jac
         stacked = jnp.stack(basis)
         local_dots = jnp.sum(stacked * vector[None], axis=(1, 2, 3))
-        dots, before = lax.psum((local_dots, jnp.sum(vector * vector)), ("row", "col"))
+        dots, before = lax.psum(lax.psum((local_dots, jnp.sum(vector * vector)), "col"), "row")
         vector = vector - jnp.sum(dots[:, None, None, None] * stacked, axis=0)
         squared = before - jnp.sum(dots * dots)
         size_new = jnp.sqrt(squared + tiny_eps)

time: 281 us -> 236 us (0.84)
  blocking collectives: 156 us -> 111 us
    psum x4 -> x8, blocking collectives: 123 us -> 77.6 us  [the longest x4 43.9 us: body(): lax.psum(lax.psum((local_dots, jnp.sum(vector * vector)), 'col'), 'row')]
  transfers between devices with their start and end apart: 20 -> 20, of which waited for: 5 -> 5; matrix products, arithmetic and copies ran while one was open for 5% -> 6% of each run, Pallas kernels for 0% -> 0%
where the time goes in v1:
time: 236 us; the launch traced here: 234 us
  blocking collectives  111 us (47%)
  starting transfers between devices  52 us (22%)
  between operations  33.7 us (14%)
  other arithmetic  19.4 us (8%)
  local copies, waits for them, and re-layouts  15 us (6%)
  waiting for transfers between devices  3.3 us (1%)
    psum x4, blocking collectives, body(): lax.psum(lax.psum((local_dots, jnp.sum(vector * vector)), 'col'), 'row')  43.9 us
    ppermute x10, starting transfers between devices, extended(): lax.ppermute(lax.slice_in_dim(block, block.shape[dim] - width, None, axis...  39 us
    psum x4, blocking collectives, body(): lax.psum((local_dots, jnp.sum(vector * vector)), 'col')  33.7 us
    psum x1, blocking collectives, body(): beta = jnp.sqrt(lax.psum(jnp.sum(rhs * rhs), ('row', 'col')) + tiny_eps)  33 us
    ppermute x10, starting transfers between devices, extended(): lax.ppermute(lax.slice_in_dim(block, 0, width, axis=dim), axis, backward)  13 us
    another operation x8, other arithmetic  7.82 us
    scatter x8, local copies, waits for them, and re-layouts, body(): hessen.at[:index + 1, index].set(dots).at[index + 1, index].set(size_new)  5.25 us
  transfers between devices with their start and end apart: 20, of which 5 were waited for; matrix products, arithmetic and copies ran while one was open for 6% of the time, Pallas kernels for 0%

profile of v1, /device:TPU:0, one launch (start us, length us, event | category | flops | bytes accessed | tf_op | source)
XLA Modules:
  0.0 234.1 jit_solution(16033318331616442864)
XLA Ops:
  0.6 0.8 fusion.64
  1.4 1.3 collective-permute-start
  2.7 5.6 %collective-permute-start.1 = (f32[10,1,128]{2,1,0:T(1,128)S(1)}, f32[10,1,128]{2,1,0:T(1,128)S(1)}, u32[]{:S(2)}, u32[]{:S(2)}) collective-permute-start(f32[10,1,128]{2,1,0:T(1,128)S(1)} %get-tuple-element.396), channel_id=1, source_target_pairs={{0,4},{4,8},{8,12},{1,5},{5,9},{9,13},{2,6},{6,10},{10,14},{3,7},{... | collective-permute-start | bytes 15368 | tf_op jit(solution)/shard_map/ppermute | solution.py:16
  8.4 1.3 multiply_reduce_fusion.9
  10.3 0.7 and_reduce_fusion.1
  11.0 0.7 and_reduce_fusion
  12.5 1.3 collective-permute-start.2
  13.8 3.0 %collective-permute-start.3 = (f32[10,18,1]{2,1,0:T(8,128)S(1)}, f32[10,18,1]{2,1,0:T(8,128)S(1)}, u32[]{:S(2)}, u32[]{:S(2)}) collective-permute-start(f32[10,18,1]{2,1,0:T(8,128)S(1)} %get-tuple-element.387), channel_id=1, source_target_pairs={{0,1},{1,2},{2,3},{4,5},{5,6},{6,7},{8,9},{9,10},{10,11},{12,13},{... | collective-permute-start | bytes 2168 | tf_op jit(solution)/shard_map/ppermute | solution.py:16
  16.9 0.9 collective-permute-done.3
  17.8 0.8 multiply_reduce_fusion.21
  18.6 33.0 %psum.119 = f32[]{:T(128)} all-reduce(f32[]{:T(128)} %get-tuple-element.376), channel_id=1, replica_groups=mesh['parts'=2,'row'=4,'col'=4] {'row','col'}, use_global_device_ids=true, to_apply=%region_2.0 | all-reduce | flops 1 | bytes 8 | tf_op jit(solution)/shard_map/psum | solution.py:63
  52.4 1.4 collective-permute-start.4
  53.9 4.5 %collective-permute-start.5 = (f32[10,1,128]{2,1,0:T(1,128)S(1)}, f32[10,1,128]{2,1,0:T(1,128)S(1)}, u32[]{:S(2)}, u32[]{:S(2)}) collective-permute-start(f32[10,1,128]{2,1,0:T(1,128)S(1)} %get-tuple-element.394), channel_id=1, source_target_pairs={{0,4},{4,8},{8,12},{1,5},{5,9},{9,13},{2,6},{6,10},{10,14},{3,7},{... | collective-permute-start | bytes 15368 | tf_op jit(solution)/shard_map/ppermute | solution.py:16
  59.9 1.3 collective-permute-start.6
  61.2 3.0 %collective-permute-start.7 = (f32[10,18,1]{2,1,0:T(8,128)S(1)}, f32[10,18,1]{2,1,0:T(8,128)S(1)}, u32[]{:S(2)}, u32[]{:S(2)}) collective-permute-start(f32[10,18,1]{2,1,0:T(8,128)S(1)} %get-tuple-element.385), channel_id=1, source_target_pairs={{0,1},{1,2},{2,3},{4,5},{5,6},{6,7},{8,9},{9,10},{10,11},{12,13},{... | collective-permute-start | bytes 2168 | tf_op jit(solution)/shard_map/ppermute | solution.py:16
  64.3 0.9 collective-permute-done.7
  65.2 0.8 multiply_reduce_fusion.20
  66.0 7.5 %all-reduce.6 = (f32[]{:T(128)}, f32[1]{0:T(128)}) all-reduce(f32[]{:T(128)} %get-tuple-element.351, f32[1]{0:T(128)} %bitcast.2), channel_id=1, replica_groups=mesh['parts'=2,'row'=4,'col'=4] {'col'}, use_global_device_ids=true, to_apply=%region_9.0 | all-reduce | flops 2 | bytes 16 | tf_op jit(solution)/shard_map/psum | solution.py:74
  73.4 11.3 %all-reduce.10 = (f32[]{:T(128)}, f32[1]{0:T(128)}) all-reduce(f32[]{:T(128)} %get-tuple-element.358, f32[1]{0:T(128)} %get-tuple-element.359), channel_id=1, replica_groups=mesh['parts'=2,'row'=4,'col'=4] {'row'}, use_global_device_ids=true, to_apply=%region_10.0 | all-reduce | flops 2 | bytes 16 | tf_op jit(solution)/shard_map/psum | solution.py:74
  87.5 1.3 collective-permute-start.8
  88.8 4.5 %collective-permute-start.9 = (f32[10,1,128]{2,1,0:T(1,128)S(1)}, f32[10,1,128]{2,1,0:T(1,128)S(1)}, u32[]{:S(2)}, u32[]{:S(2)}) collective-permute-start(f32[10,1,128]{2,1,0:T(1,128)S(1)} %get-tuple-element.392), channel_id=1, source_target_pairs={{0,4},{4,8},{8,12},{1,5},{5,9},{9,13},{2,6},{6,10},{10,14},{3,7},{... | collective-permute-start | bytes 15368 | tf_op jit(solution)/shard_map/ppermute | solution.py:16
  93.4 1.3 collective-permute-done.9
  94.8 1.3 collective-permute-start.10
  96.1 3.0 %collective-permute-start.11 = (f32[10,18,1]{2,1,0:T(8,128)S(1)}, f32[10,18,1]{2,1,0:T(8,128)S(1)}, u32[]{:S(2)}, u32[]{:S(2)}) collective-permute-start(f32[10,18,1]{2,1,0:T(8,128)S(1)} %get-tuple-element.383), channel_id=1, source_target_pairs={{0,1},{1,2},{2,3},{4,5},{5,6},{6,7},{8,9},{9,10},{10,11},{12,13},{... | collective-permute-start | bytes 2168 | tf_op jit(solution)/shard_map/ppermute | solution.py:16
  100.1 0.8 multiply_reduce_fusion.18
  101.0 9.2 %all-reduce.5 = (f32[2]{0:T(128)S(1)}, f32[]{:T(128)}) all-reduce(f32[2]{0:T(128)S(1)} %multiply_reduce_fusion.15, f32[]{:T(128)} %get-tuple-element.372), channel_id=1, replica_groups=mesh['parts'=2,'row'=4,'col'=4] {'col'}, use_global_device_ids=true, to_apply=%region_15.0 | all-reduce | flops 3 | bytes 24 | tf_op jit(solution)/shard_map/psum | solution.py:74
  110.2 11.2 %all-reduce.9 = (f32[2]{0:T(128)S(1)}, f32[]{:T(128)}) all-reduce(f32[2]{0:T(128)S(1)} %get-tuple-element.356, f32[]{:T(128)} %get-tuple-element.357), channel_id=1, replica_groups=mesh['parts'=2,'row'=4,'col'=4] {'row'}, use_global_device_ids=true, to_apply=%region_16.0 | all-reduce | flops 3 | bytes 24 | tf_op jit(solution)/shard_map/psum | solution.py:74
  123.7 1.3 collective-permute-start.12
  125.0 4.5 %collective-permute-start.13 = (f32[10,1,128]{2,1,0:T(1,128)S(1)}, f32[10,1,128]{2,1,0:T(1,128)S(1)}, u32[]{:S(2)}, u32[]{:S(2)}) collective-permute-start(f32[10,1,128]{2,1,0:T(1,128)S(1)} %get-tuple-element.390), channel_id=1, source_target_pairs={{0,4},{4,8},{8,12},{1,5},{5,9},{9,13},{2,6},{6,10},{10,14},{3,7},{... | collective-permute-start | bytes 15368 | tf_op jit(solution)/shard_map/ppermute | solution.py:16
  129.5 1.9 broadcast_select_fusion.2
  131.5 1.3 collective-permute-start.14
  132.8 3.0 %collective-permute-start.15 = (f32[10,18,1]{2,1,0:T(8,128)S(1)}, f32[10,18,1]{2,1,0:T(8,128)S(1)}, u32[]{:S(2)}, u32[]{:S(2)}) collective-permute-start(f32[10,18,1]{2,1,0:T(8,128)S(1)} %get-tuple-element.381), channel_id=1, source_target_pairs={{0,1},{1,2},{2,3},{4,5},{5,6},{6,7},{8,9},{9,10},{10,11},{12,13},{... | collective-permute-start | bytes 2168 | tf_op jit(solution)/shard_map/ppermute | solution.py:16
  135.9 1.4 scatter.60
  137.5 0.8 multiply_reduce_fusion.17
  138.4 8.5 %all-reduce.4 = (f32[3]{0:T(128)S(1)}, f32[]{:T(128)}) all-reduce(f32[3]{0:T(128)S(1)} %multiply_reduce_fusion.13, f32[]{:T(128)} %get-tuple-element.370), channel_id=1, replica_groups=mesh['parts'=2,'row'=4,'col'=4] {'col'}, use_global_device_ids=true, to_apply=%region_26.0 | all-reduce | flops 4 | bytes 32 | tf_op jit(solution)/shard_map/psum | solution.py:74
  146.9 10.7 %all-reduce.8 = (f32[3]{0:T(128)S(1)}, f32[]{:T(128)}) all-reduce(f32[3]{0:T(128)S(1)} %get-tuple-element.354, f32[]{:T(128)} %get-tuple-element.355), channel_id=1, replica_groups=mesh['parts'=2,'row'=4,'col'=4] {'row'}, use_global_device_ids=true, to_apply=%region_27.0 | all-reduce | flops 4 | bytes 32 | tf_op jit(solution)/shard_map/psum | solution.py:74
  159.7 1.3 collective-permute-start.16
  161.0 4.5 %collective-permute-start.17 = (f32[10,1,128]{2,1,0:T(1,128)S(1)}, f32[10,1,128]{2,1,0:T(1,128)S(1)}, u32[]{:S(2)}, u32[]{:S(2)}) collective-permute-start(f32[10,1,128]{2,1,0:T(1,128)S(1)} %get-tuple-element.388), channel_id=1, source_target_pairs={{0,4},{4,8},{8,12},{1,5},{5,9},{9,13},{2,6},{6,10},{10,14},{3,7},{... | collective-permute-start | bytes 15368 | tf_op jit(solution)/shard_map/ppermute | solution.py:16
  165.5 1.9 broadcast_select_fusion.1
  167.6 1.3 collective-permute-start.18
  168.9 3.0 %collective-permute-start.19 = (f32[10,18,1]{2,1,0:T(8,128)S(1)}, f32[10,18,1]{2,1,0:T(8,128)S(1)}, u32[]{:S(2)}, u32[]{:S(2)}) collective-permute-start(f32[10,18,1]{2,1,0:T(8,128)S(1)} %get-tuple-element.379), channel_id=1, source_target_pairs={{0,1},{1,2},{2,3},{4,5},{5,6},{6,7},{8,9},{9,10},{10,11},{12,13},{... | collective-permute-start | bytes 2168 | tf_op jit(solution)/shard_map/ppermute | solution.py:16
  172.0 1.4 scatter.64
  173.5 0.8 multiply_reduce_fusion.16
  174.4 8.6 %all-reduce.3 = (f32[4]{0:T(128)S(1)}, f32[]{:T(128)}) all-reduce(f32[4]{0:T(128)S(1)} %multiply_reduce_fusion.11, f32[]{:T(128)} %get-tuple-element.368), channel_id=1, replica_groups=mesh['parts'=2,'row'=4,'col'=4] {'col'}, use_global_device_ids=true, to_apply=%region_37.0 | all-reduce | flops 5 | bytes 40 | tf_op jit(solution)/shard_map/psum | solution.py:74
  183.0 10.6 %all-reduce.7 = (f32[4]{0:T(128)S(1)}, f32[]{:T(128)}) all-reduce(f32[4]{0:T(128)S(1)} %get-tuple-element.352, f32[]{:T(128)} %get-tuple-element.353), channel_id=1, replica_groups=mesh['parts'=2,'row'=4,'col'=4] {'row'}, use_global_device_ids=true, to_apply=%region_38.0 | all-reduce | flops 5 | bytes 40 | tf_op jit(solution)/shard_map/psum | solution.py:74
  195.6 2.0 broadcast_select_fusion
  197.6 1.3 scatter.66
  227.4 0.7 multiply_reduce_fusion.23
  (111 shorter events, 16.5 us)
Async XLA Ops:
  1.4 10.9 %collective-permute-start = (f32[10,1,128]{2,1,0:T(1,128)S(1)}, f32[10,1,128]{2,1,0:T(1,128)S(1)}, u32[]{:S(2)}, u32[]{:S(2)}) collective-permute-start(f32[10,1,128]{2,1,0:T(1,128)S(1)} %get-tuple-element.397), channel_id=1, source_target_pairs={{4,0},{8,4},{12,8},{5,1},{9,5},{13,9},{6,2},{10,6},{14,10},{7,3},{... | collective-permute-start | bytes 15368 | tf_op jit(solution)/shard_map/ppermute | solution.py:19
  2.7 5.6 %copy-start.5 = (f32[10,2]{0,1:T(2,128)S(1)}, f32[10,2]{0,1:T(2,128)}, u32[]{:S(2)}) copy-start(f32[10,2]{0,1:T(2,128)} %param.68) | copy-start | bytes 244
  2.7 9.6 %collective-permute-start.1 = (f32[10,1,128]{2,1,0:T(1,128)S(1)}, f32[10,1,128]{2,1,0:T(1,128)S(1)}, u32[]{:S(2)}, u32[]{:S(2)}) collective-permute-start(f32[10,1,128]{2,1,0:T(1,128)S(1)} %get-tuple-element.396), channel_id=1, source_target_pairs={{0,4},{4,8},{8,12},{1,5},{5,9},{9,13},{2,6},{6,10},{10,14},{3,7},{... | collective-permute-start | bytes 15368 | tf_op jit(solution)/shard_map/ppermute | solution.py:16
  8.4 2.0 copy-start.6
  8.4 2.7 %copy-start.7 = (s32[2]{0:T(128)S(1)}, s32[2]{0:T(128)}, u32[]{:S(2)}) copy-start(s32[2]{0:T(128)} %constant.663.clone.1) | copy-start | bytes 28
  8.4 4.0 %copy-start.2 = (f32[10,16,128]{2,1,0:T(8,128)S(1)}, f32[10,16,128]{2,1,0:T(8,128)}, u32[]{:S(2)}) copy-start(f32[10,16,128]{2,1,0:T(8,128)} %param.64) | copy-start | bytes 245764
  8.4 9.4 %copy-start.3 = (f32[10,16,128]{2,1,0:T(8,128)S(1)}, f32[10,16,128]{2,1,0:T(8,128)}, u32[]{:S(2)}) copy-start(f32[10,16,128]{2,1,0:T(8,128)} %param.67) | copy-start | bytes 245764
  8.4 9.4 %copy-start.4 = (f32[10,16,128]{2,1,0:T(8,128)S(1)}, f32[10,16,128]{2,1,0:T(8,128)}, u32[]{:S(2)}) copy-start(f32[10,16,128]{2,1,0:T(8,128)} %param.65) | copy-start | bytes 245764
  9.7 42.6 %copy-start.1 = (f32[10,10,16,128]{3,2,1,0:T(8,128)S(1)}, f32[10,10,16,128]{3,2,1,0:T(8,128)}, u32[]{:S(2)}) copy-start(f32[10,10,16,128]{3,2,1,0:T(8,128)} %param.69) | copy-start | bytes 2457604
  12.5 4.4 %collective-permute-start.2 = (f32[10,18,1]{2,1,0:T(8,128)S(1)}, f32[10,18,1]{2,1,0:T(8,128)S(1)}, u32[]{:S(2)}, u32[]{:S(2)}) collective-permute-start(f32[10,18,1]{2,1,0:T(8,128)S(1)} %get-tuple-element.386), channel_id=1, source_target_pairs={{1,0},{2,1},{3,2},{5,4},{6,5},{7,6},{9,8},{10,9},{11,10},{13,12},{... | collective-permute-start | bytes 2168 | tf_op jit(solution)/shard_map/ppermute | solution.py:19
  13.8 4.0 %collective-permute-start.3 = (f32[10,18,1]{2,1,0:T(8,128)S(1)}, f32[10,18,1]{2,1,0:T(8,128)S(1)}, u32[]{:S(2)}, u32[]{:S(2)}) collective-permute-start(f32[10,18,1]{2,1,0:T(8,128)S(1)} %get-tuple-element.387), channel_id=1, source_target_pairs={{0,1},{1,2},{2,3},{4,5},{5,6},{6,7},{8,9},{9,10},{10,11},{12,13},{... | collective-permute-start | bytes 2168 | tf_op jit(solution)/shard_map/ppermute | solution.py:16
  52.3 11.9 %copy-start = (f32[10,10,16,128]{3,2,1,0:T(8,128)S(1)}, f32[10,10,16,128]{3,2,1,0:T(8,128)}, u32[]{:S(2)}) copy-start(f32[10,10,16,128]{3,2,1,0:T(8,128)} %param.66) | copy-start | bytes 2457604
  52.4 7.2 %collective-permute-start.4 = (f32[10,1,128]{2,1,0:T(1,128)S(1)}, f32[10,1,128]{2,1,0:T(1,128)S(1)}, u32[]{:S(2)}, u32[]{:S(2)}) collective-permute-start(f32[10,1,128]{2,1,0:T(1,128)S(1)} %get-tuple-element.395), channel_id=1, source_target_pairs={{4,0},{8,4},{12,8},{5,1},{9,5},{13,9},{6,2},{10,6},{14,10},{7,3},{... | collective-permute-start | bytes 15368 | tf_op jit(solution)/shard_map/ppermute | solution.py:19
  53.9 5.9 %collective-permute-start.5 = (f32[10,1,128]{2,1,0:T(1,128)S(1)}, f32[10,1,128]{2,1,0:T(1,128)S(1)}, u32[]{:S(2)}, u32[]{:S(2)}) collective-permute-start(f32[10,1,128]{2,1,0:T(1,128)S(1)} %get-tuple-element.394), channel_id=1, source_target_pairs={{0,4},{4,8},{8,12},{1,5},{5,9},{9,13},{2,6},{6,10},{10,14},{3,7},{... | collective-permute-start | bytes 15368 | tf_op jit(solution)/shard_map/ppermute | solution.py:16
  59.9 4.4 %collective-permute-start.6 = (f32[10,18,1]{2,1,0:T(8,128)S(1)}, f32[10,18,1]{2,1,0:T(8,128)S(1)}, u32[]{:S(2)}, u32[]{:S(2)}) collective-permute-start(f32[10,18,1]{2,1,0:T(8,128)S(1)} %get-tuple-element.384), channel_id=1, source_target_pairs={{1,0},{2,1},{3,2},{5,4},{6,5},{7,6},{9,8},{10,9},{11,10},{13,12},{... | collective-permute-start | bytes 2168 | tf_op jit(solution)/shard_map/ppermute | solution.py:19
  61.2 4.0 %collective-permute-start.7 = (f32[10,18,1]{2,1,0:T(8,128)S(1)}, f32[10,18,1]{2,1,0:T(8,128)S(1)}, u32[]{:S(2)}, u32[]{:S(2)}) collective-permute-start(f32[10,18,1]{2,1,0:T(8,128)S(1)} %get-tuple-element.385), channel_id=1, source_target_pairs={{0,1},{1,2},{2,3},{4,5},{5,6},{6,7},{8,9},{9,10},{10,11},{12,13},{... | collective-permute-start | bytes 2168 | tf_op jit(solution)/shard_map/ppermute | solution.py:16
  87.5 5.9 %collective-permute-start.8 = (f32[10,1,128]{2,1,0:T(1,128)S(1)}, f32[10,1,128]{2,1,0:T(1,128)S(1)}, u32[]{:S(2)}, u32[]{:S(2)}) collective-permute-start(f32[10,1,128]{2,1,0:T(1,128)S(1)} %get-tuple-element.393), channel_id=1, source_target_pairs={{4,0},{8,4},{12,8},{5,1},{9,5},{13,9},{6,2},{10,6},{14,10},{7,3},{... | collective-permute-start | bytes 15368 | tf_op jit(solution)/shard_map/ppermute | solution.py:19
  88.8 5.9 %collective-permute-start.9 = (f32[10,1,128]{2,1,0:T(1,128)S(1)}, f32[10,1,128]{2,1,0:T(1,128)S(1)}, u32[]{:S(2)}, u32[]{:S(2)}) collective-permute-start(f32[10,1,128]{2,1,0:T(1,128)S(1)} %get-tuple-element.392), channel_id=1, source_target_pairs={{0,4},{4,8},{8,12},{1,5},{5,9},{9,13},{2,6},{6,10},{10,14},{3,7},{... | collective-permute-start | bytes 15368 | tf_op jit(solution)/shard_map/ppermute | solution.py:16
  94.8 5.2 %collective-permute-start.10 = (f32[10,18,1]{2,1,0:T(8,128)S(1)}, f32[10,18,1]{2,1,0:T(8,128)S(1)}, u32[]{:S(2)}, u32[]{:S(2)}) collective-permute-start(f32[10,18,1]{2,1,0:T(8,128)S(1)} %get-tuple-element.382), channel_id=1, source_target_pairs={{1,0},{2,1},{3,2},{5,4},{6,5},{7,6},{9,8},{10,9},{11,10},{13,12},{... | collective-permute-start | bytes 2168 | tf_op jit(solution)/shard_map/ppermute | solution.py:19
  96.1 4.0 %collective-permute-start.11 = (f32[10,18,1]{2,1,0:T(8,128)S(1)}, f32[10,18,1]{2,1,0:T(8,128)S(1)}, u32[]{:S(2)}, u32[]{:S(2)}) collective-permute-start(f32[10,18,1]{2,1,0:T(8,128)S(1)} %get-tuple-element.383), channel_id=1, source_target_pairs={{0,1},{1,2},{2,3},{4,5},{5,6},{6,7},{8,9},{9,10},{10,11},{12,13},{... | collective-permute-start | bytes 2168 | tf_op jit(solution)/shard_map/ppermute | solution.py:16
  123.7 7.7 %collective-permute-start.12 = (f32[10,1,128]{2,1,0:T(1,128)S(1)}, f32[10,1,128]{2,1,0:T(1,128)S(1)}, u32[]{:S(2)}, u32[]{:S(2)}) collective-permute-start(f32[10,1,128]{2,1,0:T(1,128)S(1)} %get-tuple-element.391), channel_id=1, source_target_pairs={{4,0},{8,4},{12,8},{5,1},{9,5},{13,9},{6,2},{10,6},{14,10},{7,3},{... | collective-permute-start | bytes 15368 | tf_op jit(solution)/shard_map/ppermute | solution.py:19
  125.0 6.4 %collective-permute-start.13 = (f32[10,1,128]{2,1,0:T(1,128)S(1)}, f32[10,1,128]{2,1,0:T(1,128)S(1)}, u32[]{:S(2)}, u32[]{:S(2)}) collective-permute-start(f32[10,1,128]{2,1,0:T(1,128)S(1)} %get-tuple-element.390), channel_id=1, source_target_pairs={{0,4},{4,8},{8,12},{1,5},{5,9},{9,13},{2,6},{6,10},{10,14},{3,7},{... | collective-permute-start | bytes 15368 | tf_op jit(solution)/shard_map/ppermute | solution.py:16
  131.5 6.0 %collective-permute-start.14 = (f32[10,18,1]{2,1,0:T(8,128)S(1)}, f32[10,18,1]{2,1,0:T(8,128)S(1)}, u32[]{:S(2)}, u32[]{:S(2)}) collective-permute-start(f32[10,18,1]{2,1,0:T(8,128)S(1)} %get-tuple-element.380), channel_id=1, source_target_pairs={{1,0},{2,1},{3,2},{5,4},{6,5},{7,6},{9,8},{10,9},{11,10},{13,12},{... | collective-permute-start | bytes 2168 | tf_op jit(solution)/shard_map/ppermute | solution.py:19
  132.8 4.7 %collective-permute-start.15 = (f32[10,18,1]{2,1,0:T(8,128)S(1)}, f32[10,18,1]{2,1,0:T(8,128)S(1)}, u32[]{:S(2)}, u32[]{:S(2)}) collective-permute-start(f32[10,18,1]{2,1,0:T(8,128)S(1)} %get-tuple-element.381), channel_id=1, source_target_pairs={{0,1},{1,2},{2,3},{4,5},{5,6},{6,7},{8,9},{9,10},{10,11},{12,13},{... | collective-permute-start | bytes 2168 | tf_op jit(solution)/shard_map/ppermute | solution.py:16
  159.7 7.8 %collective-permute-start.16 = (f32[10,1,128]{2,1,0:T(1,128)S(1)}, f32[10,1,128]{2,1,0:T(1,128)S(1)}, u32[]{:S(2)}, u32[]{:S(2)}) collective-permute-start(f32[10,1,128]{2,1,0:T(1,128)S(1)} %get-tuple-element.389), channel_id=1, source_target_pairs={{4,0},{8,4},{12,8},{5,1},{9,5},{13,9},{6,2},{10,6},{14,10},{7,3},{... | collective-permute-start | bytes 15368 | tf_op jit(solution)/shard_map/ppermute | solution.py:19
  161.0 6.5 %collective-permute-start.17 = (f32[10,1,128]{2,1,0:T(1,128)S(1)}, f32[10,1,128]{2,1,0:T(1,128)S(1)}, u32[]{:S(2)}, u32[]{:S(2)}) collective-permute-start(f32[10,1,128]{2,1,0:T(1,128)S(1)} %get-tuple-element.388), channel_id=1, source_target_pairs={{0,4},{4,8},{8,12},{1,5},{5,9},{9,13},{2,6},{6,10},{10,14},{3,7},{... | collective-permute-start | bytes 15368 | tf_op jit(solution)/shard_map/ppermute | solution.py:16
  167.6 5.9 %collective-permute-start.18 = (f32[10,18,1]{2,1,0:T(8,128)S(1)}, f32[10,18,1]{2,1,0:T(8,128)S(1)}, u32[]{:S(2)}, u32[]{:S(2)}) collective-permute-start(f32[10,18,1]{2,1,0:T(8,128)S(1)} %get-tuple-element.378), channel_id=1, source_target_pairs={{1,0},{2,1},{3,2},{5,4},{6,5},{7,6},{9,8},{10,9},{11,10},{13,12},{... | collective-permute-start | bytes 2168 | tf_op jit(solution)/shard_map/ppermute | solution.py:19
  168.9 4.6 %collective-permute-start.19 = (f32[10,18,1]{2,1,0:T(8,128)S(1)}, f32[10,18,1]{2,1,0:T(8,128)S(1)}, u32[]{:S(2)}, u32[]{:S(2)}) collective-permute-start(f32[10,18,1]{2,1,0:T(8,128)S(1)} %get-tuple-element.379), channel_id=1, source_target_pairs={{0,1},{1,2},{2,3},{4,5},{5,6},{6,7},{8,9},{9,10},{10,11},{12,13},{... | collective-permute-start | bytes 2168 | tf_op jit(solution)/shard_map/ppermute | solution.py:16
